TPU v7x, 16 devices: a whole 2x2x2 slice. The times are simulated.
16 devices in a mesh: rep: 1, dp: 16 (over x, y, z, core).
Axes of the slice: x: 2, y: 2, z: 2, core: 2. Of those that a mesh axis runs over, the one named last changes fastest.
Arguments:
- x: bfloat16 [16, 2048, 1024], P(('rep', 'dp'))
- dy: bfloat16 [16, 2048, 1024], P(('rep', 'dp'))
- w_gate: bfloat16 [2, 1024, 3328], P(None, 'dp')
- w_up: bfloat16 [2, 1024, 3328], P(None, 'dp')
- w_down: bfloat16 [2, 3328, 1024], P(None, 'dp')
- m_w_gate: float32 [2, 1024, 3328], P(None, 'dp')
- m_w_up: float32 [2, 1024, 3328], P(None, 'dp')
- m_w_down: float32 [2, 3328, 1024], P(None, 'dp')
- v_w_gate: float32 [2, 1024, 3328], P(None, 'dp')
- v_w_up: float32 [2, 1024, 3328], P(None, 'dp')
- v_w_down: float32 [2, 3328, 1024], P(None, 'dp')
Outputs:
- output 1: bfloat16 [2, 1024, 3328], P('rep', 'dp')
- output 2: bfloat16 [2, 1024, 3328], P('rep', 'dp')
- output 3: bfloat16 [2, 3328, 1024], P('rep', 'dp')
- output 4: float32 [2, 1024, 3328], P('rep', 'dp')
- output 5: float32 [2, 1024, 3328], P('rep', 'dp')
- output 6: float32 [2, 3328, 1024], P('rep', 'dp')
- output 7: float32 [2, 1024, 3328], P('rep', 'dp')
- output 8: float32 [2, 1024, 3328], P('rep', 'dp')
- output 9: float32 [2, 3328, 1024], P('rep', 'dp')
All inputs are finite; a program needn't handle non-finite values.
Results may differ from a plain program's by a relative error of at most 0.0224.
Values are sent between devices in bfloat16 or wider.
A program may use at most 2 GiB of HBM per device.

v0:
```python
import jax
import jax.numpy as jnp
from jax import lax
from jax.sharding import PartitionSpec as P

NAMES = ("w_gate", "w_up", "w_down")


def matmul(a, w):
    return jnp.dot(a, w, preferred_element_type=jnp.float32).astype(jnp.bfloat16)


def normed(h):
    wide = h.astype(jnp.float32)
    scale = lax.rsqrt(jnp.mean(wide**2, -1, keepdims=True) + 1e-6)
    return (wide * scale).astype(jnp.bfloat16)


def layer(h, w):
    a = normed(h)
    gate = jnp.dot(a, w["w_gate"], preferred_element_type=jnp.float32)
    up = jnp.dot(a, w["w_up"], preferred_element_type=jnp.float32)
    return h + matmul((jax.nn.silu(gate) * up).astype(jnp.bfloat16), w["w_down"])


def adamw(w, m, v, g):
    m = 0.9 * m + 0.1 * g
    v = 0.95 * v + 0.05 * g * g
    step = m * lax.rsqrt(v + 1e-8) + 0.1 * w
    return (w - 0.02 * step).astype(jnp.bfloat16), m, v


def clipped(gradients, sum_of_squares, count):
    factor = jnp.minimum(1.0, 0.5 * lax.rsqrt(sum_of_squares / count + 1e-30))
    return [g * factor for g in gradients]


def solution(mesh):
    def fetched(weights, number):
        return {name: lax.all_gather(w[number], "dp", axis=0, tiled=True) for name, w in zip(NAMES, weights, strict=True)}

    def step(x, dy, *arrays):
        weights, m, v = (arrays[i : i + 3] for i in (0, 3, 6))
        layers = weights[0].shape[0]
        h, kept = x[0], []
        for number in range(layers):
            kept.append(h)
            h = layer(h, fetched(weights, number))
        by_h, mine = dy[0], [None] * layers
        for number in reversed(range(layers)):
            _, back = jax.vjp(lambda w, h: layer(h, w), fetched(weights, number), kept[number])
            by_w, by_h = back(by_h)
            mine[number] = [lax.psum_scatter(by_w[name], "dp", scatter_dimension=0, tiled=True) for name in NAMES]
        gradients = [jnp.stack([mine[number][i] for number in range(layers)]).astype(jnp.float32) for i in range(3)]
        squares = lax.psum(sum(jnp.sum(g * g) for g in gradients), "dp")
        gradients = clipped(gradients, squares, lax.psum(1, "dp") * sum(g.size for g in gradients))
        new = [adamw(w.astype(jnp.float32), m, v, g) for w, m, v, g in zip(weights, m, v, gradients, strict=True)]
        return tuple(one[which] for which in range(3) for one in new)

    states, cut = P(("rep", "dp"), None, None), P(None, "dp", None)
    return jax.shard_map(
        step,
        mesh=mesh,
        in_specs=(states, states) + (cut,) * 9,
        out_specs=(P("rep", "dp", None),) * 9,
        check_vma=False,
    )
```

profile of v0, /device:TPU:0, one launch (start us, length us, event | category | flops | bytes accessed | tf_op | source)
XLA Modules:
  0.0 944.3 jit_solution(15054364251376965153)
XLA Ops:
  15.5 6.5 copy.20
  25.1 6.5 copy.21
  31.6 25.6 %all-gather.13.cloned.1.call-done = bf16[1,1024,3328]{2,1,0:T(8,128)(2,1)} async-done(((bf16[1,64,3328]{2,1,0:T(8,128)(2,1)}), bf16[1,1024,3328]{2,1,0:T(8,128)(2,1)}) %all-gather.13.cloned.1.call-update) | async-done | bytes 6815760 | tf_op jit(solution)/shard_map/all_gather | solution.py:40
  57.2 23.2 %fusion.41 = f32[2048,3328]{1,0:T(8,128)} fusion(bf16[1,1024,3328]{2,1,0:T(8,128)(2,1)} %all-gather.13.cloned.1.call-done, bf16[1,2048,1024]{1,2,0:T(8,128)(2,1)} %copy.20, f32[2048]{0:T(1024)S(1)} %add_rsqrt_fusion), kind=kOutput, calls=%fused_computation.59 | convolution fusion | flops 13964935168 | bytes 38281216 | tf_op jit(solution)/shard_map/dot_general | solution.py:21
  80.4 23.2 %all-gather.15.cloned.1.call-done = bf16[1,1024,3328]{2,1,0:T(8,128)(2,1)} async-done(((bf16[1,64,3328]{2,1,0:T(8,128)(2,1)}), bf16[1,1024,3328]{2,1,0:T(8,128)(2,1)}) %all-gather.15.cloned.1.call-update) | async-done | bytes 6815760 | tf_op jit(solution)/shard_map/all_gather | solution.py:40
  103.5 32.1 %multiply_convert_fusion.1 = (bf16[2048,3328]{1,0:T(8,128)(2,1)}, f32[2048,3328]{1,0:T(8,128)}) fusion(f32[2048,3328]{1,0:T(8,128)} %fusion.41, bf16[1,1024,3328]{2,1,0:T(8,128)(2,1)} %all-gather.15.cloned.1.call-done, bf16[1,2048,1024]{1,2,0:T(8,128)(2,1)} %copy.20, f32[2048]{0:T(1024)S(1)} %add_rsqrt_fusion), kind=kOutput, calls=%fused_computation.17 | convolution fusion | flops 14005829632 | bytes 79175680 | tf_op jit(solution)/shard_map/dot_general | solution.py:22
  135.6 14.3 %all-gather.17.cloned.1.call-done = bf16[1,3328,1024]{2,1,0:T(8,128)(2,1)} async-done(((bf16[1,208,1024]{2,1,0:T(8,128)(2,1)}), bf16[1,3328,1024]{2,1,0:T(8,128)(2,1)}) %all-gather.17.cloned.1.call-update) | async-done | bytes 6815760 | tf_op jit(solution)/shard_map/all_gather | solution.py:40
  149.9 22.1 %fusion.19 = (f32[2048]{0:T(1024)S(1)}, bf16[2048,1024]{0,1:T(8,128)(2,1)}) fusion(bf16[2048,3328]{1,0:T(8,128)(2,1)} %get-tuple-element.24, bf16[1,3328,1024]{2,1,0:T(8,128)(2,1)} %all-gather.17.cloned.1.call-done, bf16[1,2048,1024]{1,2,0:T(8,128)(2,1)} %copy.20), kind=kOutput, calls=%fused_computation.37 | convolution fusion | flops 13969127424 | bytes 28844032 | tf_op jit(solution)/shard_map/dot_general | solution.py:10
  172.0 24.1 %all-gather.23.cloned.1.call-done = bf16[1,1024,3328]{2,1,0:T(8,128)(2,1)} async-done(((bf16[1,64,3328]{2,1,0:T(8,128)(2,1)}), bf16[1,1024,3328]{2,1,0:T(8,128)(2,1)}) %all-gather.23.cloned.1.call-update) | async-done | bytes 6815760 | tf_op jit(solution)/shard_map/all_gather | solution.py:40
  196.1 23.5 %fusion.28 = f32[2048,3328]{1,0:T(8,128)} fusion(bf16[1,1024,3328]{2,1,0:T(8,128)(2,1)} %all-gather.23.cloned.1.call-done, bf16[2048,1024]{0,1:T(8,128)(2,1)} %get-tuple-element.27, f32[2048]{0:T(1024)S(1)} %fusion.80), kind=kOutput, calls=%fused_computation.46 | convolution fusion | flops 13964935168 | bytes 38281216 | tf_op jit(solution)/shard_map/jvp()/dot_general | solution.py:22
  219.6 22.7 %all-gather.21.cloned.1.call-done = bf16[1,3328,1024]{2,1,0:T(8,128)(2,1)} async-done(((bf16[1,208,1024]{2,1,0:T(8,128)(2,1)}), bf16[1,3328,1024]{2,1,0:T(8,128)(2,1)}) %all-gather.21.cloned.1.call-update) | async-done | bytes 6815760 | tf_op jit(solution)/shard_map/all_gather | solution.py:40
  242.3 21.0 %convolution_convert_fusion.1 = bf16[2048,3328]{1,0:T(8,128)(2,1)} fusion(bf16[1,3328,1024]{2,1,0:T(8,128)(2,1)} %all-gather.21.cloned.1.call-done, bf16[1,2048,1024]{2,1,0:T(8,128)(2,1)} %param.12), kind=kOutput, calls=%fused_computation.23 | convolution fusion | flops 13965459456 | bytes 24641536 | tf_op jit(solution)/shard_map/transpose(jvp())/dot_general | solution.py:10
  263.3 25.2 %all-gather.19.cloned.1.call-done = bf16[1,1024,3328]{2,1,0:T(8,128)(2,1)} async-done(((bf16[1,64,3328]{2,1,0:T(8,128)(2,1)}), bf16[1,1024,3328]{2,1,0:T(8,128)(2,1)}) %all-gather.19.cloned.1.call-update) | async-done | bytes 6815760 | tf_op jit(solution)/shard_map/all_gather | solution.py:40
  288.5 39.6 %fusion.2 = (bf16[2048,3328]{1,0:T(8,128)(2,1)}, f32[2048,3328]{1,0:T(8,128)}) fusion(f32[2048,3328]{1,0:T(8,128)} %fusion.28, bf16[2048,3328]{1,0:T(8,128)(2,1)} %convolution_convert_fusion.1, bf16[1,1024,3328]{2,1,0:T(8,128)(2,1)} %all-gather.19.cloned.1.call-done, bf16[2048,1024]{0,1:T(8,128)(2,1)} %get-tuple-element.27, f32[2048]{0:T(1024)S(1)} %fusion.80), kind=kOutput, calls=%fused_computation.8 | convolution fusion | flops 14046724096 | bytes 92807168 | tf_op jit(solution)/shard_map/jvp()/dot_general | solution.py:21
  328.1 23.1 %fusion.12 = bf16[2048,1024]{0,1:T(8,128)(2,1)} fusion(bf16[2048,3328]{1,0:T(8,128)(2,1)} %convolution_convert_fusion.1, bf16[1,1024,3328]{2,1,0:T(8,128)(2,1)} %all-gather.23.cloned.1.call-done, f32[2048,3328]{1,0:T(8,128)} %get-tuple-element.29), kind=kOutput, calls=%fused_computation.21 | convolution fusion | flops 13999538176 | bytes 51904512 | tf_op jit(solution)/shard_map/transpose(jvp())/dot_general | solution.py:22
  351.2 21.7 %fusion.21 = (f32[2048]{0:T(1024)S(1)}, bf16[2048,1024]{0,1:T(8,128)(2,1)}) fusion(bf16[2048,1024]{0,1:T(8,128)(2,1)S(1)} %copy-done.1, bf16[2048,1024]{0,1:T(8,128)(2,1)} %fusion.12, bf16[2048,3328]{1,0:T(8,128)(2,1)} %get-tuple-element.28, bf16[1,1024,3328]{2,1,0:T(8,128)(2,1)} %all-gather.19.cloned.1.call-done), kind=kOutput, calls=%fused_computation.39 | convolution fusion | flops 13969127424 | bytes 33038336 | tf_op jit(solution)/shard_map/transpose(jvp())/dot_general | solution.py:21
  373.0 4.9 fusion.44
  379.8 19.6 %convolution_convert_fusion.2 = bf16[3328,1024]{1,0:T(8,128)(2,1)} fusion(bf16[2048,3328]{1,0:T(8,128)(2,1)} %get-tuple-element.24, bf16[2048,1024]{0,1:T(8,128)(2,1)S(1)} %fusion.44), kind=kOutput, calls=%fused_computation.44 | convolution fusion | flops 13962051584 | bytes 24641536 | tf_op jit(solution)/shard_map/transpose(jvp())/dot_general | solution.py:10
  399.5 27.3 %fusion.25 = bf16[3328,1024]{1,0:T(8,128)(2,1)} fusion(f32[2048,3328]{1,0:T(8,128)} %fusion.28, bf16[1,2048,1024]{2,1,0:T(8,128)(2,1)} %param.12, f32[2048,3328]{1,0:T(8,128)} %get-tuple-element.29), kind=kOutput, calls=%fused_computation.41 | convolution fusion | flops 14002946048 | bytes 65536000 | tf_op jit(solution)/shard_map/transpose(jvp())/dot_general | solution.py:10
  426.9 21.1 %convolution_convert_fusion = bf16[2048,3328]{1,0:T(8,128)(2,1)} fusion(bf16[2048,1024]{0,1:T(8,128)(2,1)} %copy-done.2, bf16[1,3328,1024]{2,1,0:T(8,128)(2,1)} %all-gather.17.cloned.1.call-done), kind=kOutput, calls=%fused_computation.22 | convolution fusion | flops 13965459456 | bytes 24641536 | tf_op jit(solution)/shard_map/transpose(jvp())/dot_general | solution.py:10
  448.0 25.6 %fusion.27 = bf16[1024,3328]{1,0:T(8,128)(2,1)} fusion(bf16[2048,3328]{1,0:T(8,128)(2,1)} %convolution_convert_fusion, f32[2048,3328]{1,0:T(8,128)} %fusion.41, bf16[1,2048,1024]{1,2,0:T(8,128)(2,1)} %copy.20, f32[2048]{0:T(1024)S(1)} %copy-done.19), kind=kOutput, calls=%fused_computation.43 | convolution fusion | flops 14009237504 | bytes 51912704 | tf_op jit(solution)/shard_map/transpose(jvp())/dot_general | solution.py:22
  474.3 25.3 %fusion.26 = bf16[1024,3328]{1,0:T(8,128)(2,1)} fusion(bf16[2048,3328]{1,0:T(8,128)(2,1)} %convolution_convert_fusion.1, bf16[2048,1024]{0,1:T(8,128)(2,1)} %get-tuple-element.27, f32[2048]{0:T(1024)S(1)} %copy-done.15, f32[2048,3328]{1,0:T(8,128)} %get-tuple-element.29), kind=kOutput, calls=%fused_computation.42 | convolution fusion | flops 14009237504 | bytes 51912704 | tf_op jit(solution)/shard_map/transpose(jvp())/dot_general | solution.py:22
  499.7 31.2 %fusion.22 = bf16[1024,3328]{1,0:T(8,128)(2,1)} fusion(f32[2048,3328]{1,0:T(8,128)} %fusion.41, f32[2048,3328]{1,0:T(8,128)} %get-tuple-element.25, bf16[2048,3328]{1,0:T(8,128)(2,1)} %convolution_convert_fusion, bf16[1,2048,1024]{1,2,0:T(8,128)(2,1)} %copy.20, f32[2048]{0:T(1024)S(1)} %copy-done.19), kind=kOutput, calls=%fused_computation.40 | convolution fusion | flops 14043316224 | bytes 79175680 | tf_op jit(solution)/shard_map/transpose(jvp())/dot_general | solution.py:21
  531.0 21.3 %convolution_convert_fusion.3 = bf16[1024,3328]{1,0:T(8,128)(2,1)} fusion(bf16[2048,3328]{1,0:T(8,128)(2,1)} %get-tuple-element.28, bf16[2048,1024]{0,1:T(8,128)(2,1)} %get-tuple-element.27, f32[2048]{0:T(1024)S(1)} %copy-done.15), kind=kOutput, calls=%fused_computation.45 | convolution fusion | flops 13964935168 | bytes 24649728 | tf_op jit(solution)/shard_map/transpose(jvp())/dot_general | solution.py:21
  552.3 6.5 reduce-scatter.17.cloned.1.call-done
  560.9 80.4 %reduce-scatter.11.cloned.1.call-done = bf16[64,3328]{1,0:T(8,128)(2,1)} async-done(((bf16[1024,3328]{1,0:T(8,128)(2,1)}), bf16[64,3328]{1,0:T(8,128)(2,1)}) %reduce-scatter.11.cloned.1.call-update) | async-done | bytes 426000 | tf_op jit(solution)/shard_map/reduce_scatter | solution.py:53
  641.3 80.8 %reduce-scatter.13.cloned.1.call-done = bf16[64,3328]{1,0:T(8,128)(2,1)} async-done(((bf16[1024,3328]{1,0:T(8,128)(2,1)}), bf16[64,3328]{1,0:T(8,128)(2,1)}) %reduce-scatter.13.cloned.1.call-update) | async-done | bytes 426000 | tf_op jit(solution)/shard_map/reduce_scatter | solution.py:53
  724.4 80.7 %reduce-scatter.7.cloned.1.call-done = bf16[64,3328]{1,0:T(8,128)(2,1)} async-done(((bf16[1024,3328]{1,0:T(8,128)(2,1)}), bf16[64,3328]{1,0:T(8,128)(2,1)}) %reduce-scatter.7.cloned.1.call-update) | async-done | bytes 426000 | tf_op jit(solution)/shard_map/reduce_scatter | solution.py:53
  805.1 82.7 %reduce-scatter.9.cloned.1.call-done = bf16[64,3328]{1,0:T(8,128)(2,1)} async-done(((bf16[1024,3328]{1,0:T(8,128)(2,1)}), bf16[64,3328]{1,0:T(8,128)(2,1)}) %reduce-scatter.9.cloned.1.call-update) | async-done | bytes 426000 | tf_op jit(solution)/shard_map/reduce_scatter | solution.py:53
  892.0 34.0 %psum.7 = f32[]{:T(128)} all-reduce(f32[]{:T(128)S(6)} %add.99), channel_id=1, replica_groups=mesh['rep'=1,'dp'=16] {'dp'}, use_global_device_ids=true, to_apply=%region_12.13 | all-reduce | flops 1 | bytes 8 | tf_op jit(solution)/shard_map/psum | solution.py:55
  926.7 5.0 fusion.76
  932.7 4.3 fusion.67
  (75 shorter events, 21.7 us)
Async XLA Ops:
  7.2 50.0 %all-gather.13.cloned.1.call-start = ((), (), s32[]{:S(2)}) async-start(), calls=%async_computation.12 | async-start | bytes 7241728 | tf_op jit(solution)/shard_map/all_gather | solution.py:40
  9.3 94.2 %all-gather.15.cloned.1.call-start = ((), (), s32[]{:S(2)}) async-start(), calls=%async_computation.13 | async-start | bytes 7241728 | tf_op jit(solution)/shard_map/all_gather | solution.py:40
  11.5 138.4 %all-gather.17.cloned.1.call-start = ((), (), s32[]{:S(2)}) async-start(), calls=%async_computation.14 | async-start | bytes 7241728 | tf_op jit(solution)/shard_map/all_gather | solution.py:40
  13.7 182.4 %all-gather.23.cloned.1.call-start = ((), (), s32[]{:S(2)}) async-start(), calls=%async_computation.17 | async-start | bytes 7241728 | tf_op jit(solution)/shard_map/all_gather | solution.py:40
  14.2 228.0 %all-gather.21.cloned.1.call-start = ((), (), s32[]{:S(2)}) async-start(), calls=%async_computation.16 | async-start | bytes 7241728 | tf_op jit(solution)/shard_map/all_gather | solution.py:40
  14.8 273.7 %all-gather.19.cloned.1.call-start = ((), (), s32[]{:S(2)}) async-start(), calls=%async_computation.15 | async-start | bytes 7241728 | tf_op jit(solution)/shard_map/all_gather | solution.py:40
  15.4 536.9 %reduce-scatter.15.cloned.1.call-start = ((), (), s32[]{:S(2)}) async-start(), calls=%async_computation.10 | async-start | bytes 7241728 | tf_op jit(solution)/shard_map/reduce_scatter | solution.py:53
  25.1 78.5 %copy-start.18 = (f32[2048]{0:T(1024)}, f32[2048]{0:T(1024)S(1)}, u32[]{:S(2)}) copy-start(f32[2048]{0:T(1024)S(1)} %add_rsqrt_fusion) | copy-start | bytes 24580
  172.0 47.6 %copy-start.16 = (f32[2048]{0:T(1024)}, f32[2048]{0:T(1024)S(1)}, u32[]{:S(2)}) copy-start(f32[2048]{0:T(1024)S(1)} %get-tuple-element.26) | copy-start | bytes 24580
  172.0 200.9 %copy-start.14 = (f32[2048]{0:T(1024)}, f32[2048]{0:T(1024)S(1)}, u32[]{:S(2)}) copy-start(f32[2048]{0:T(1024)S(1)} %fusion.80) | copy-start | bytes 24580
  328.1 23.1 %copy-start.1 = (bf16[2048,1024]{0,1:T(8,128)(2,1)S(1)}, bf16[2048,1024]{0,1:T(8,128)(2,1)}, u32[]{:S(2)}) copy-start(bf16[2048,1024]{0,1:T(8,128)(2,1)} %get-tuple-element.27) | copy-start | bytes 12582916
  351.2 21.7 %copy-start.17 = (f32[2048]{0:T(1024)S(1)}, f32[2048]{0:T(1024)}, u32[]{:S(2)}) copy-start(f32[2048]{0:T(1024)} %copy-done.16) | copy-start | bytes 24580
  351.2 21.8 %copy-start = (bf16[1,2048,1024]{1,2,0:T(8,128)(2,1)S(1)}, bf16[1,2048,1024]{1,2,0:T(8,128)(2,1)}, u32[]{:S(2)}) copy-start(bf16[1,2048,1024]{1,2,0:T(8,128)(2,1)} %copy.21) | copy-start | bytes 12582916
  377.9 1.9 copy-start.2
  399.4 159.3 %reduce-scatter.17.cloned.1.call-start = ((), (), s32[]{:S(2)}) async-start(), calls=%async_computation.11 | async-start | bytes 7241728 | tf_op jit(solution)/shard_map/reduce_scatter | solution.py:53
  426.8 21.1 %copy-start.19 = (f32[2048]{0:T(1024)S(1)}, f32[2048]{0:T(1024)}, u32[]{:S(2)}) copy-start(f32[2048]{0:T(1024)} %copy-done.18) | copy-start | bytes 24580
  426.8 214.5 %reduce-scatter.11.cloned.1.call-start = ((), (), s32[]{:S(2)}) async-start(), calls=%async_computation.8 | async-start | bytes 7241728 | tf_op jit(solution)/shard_map/reduce_scatter | solution.py:53
  473.6 0.7 copy-start.15
  473.6 248.6 %reduce-scatter.13.cloned.1.call-start = ((), (), s32[]{:S(2)}) async-start(), calls=%async_computation.9 | async-start | bytes 7241728 | tf_op jit(solution)/shard_map/reduce_scatter | solution.py:53
  499.6 305.5 %reduce-scatter.7.cloned.1.call-start = ((), (), s32[]{:S(2)}) async-start(), calls=%async_computation.6 | async-start | bytes 7241728 | tf_op jit(solution)/shard_map/reduce_scatter | solution.py:53
  530.9 357.0 %reduce-scatter.9.cloned.1.call-start = ((), (), s32[]{:S(2)}) async-start(), calls=%async_computation.7 | async-start | bytes 7241728 | tf_op jit(solution)/shard_map/reduce_scatter | solution.py:53
  552.2 374.5 %copy-start.3 = (bf16[2,208,1024]{2,1,0:T(8,128)(2,1)S(1)}, bf16[2,208,1024]{2,1,0:T(8,128)(2,1)}, u32[]{:S(2)}) copy-start(bf16[2,208,1024]{2,1,0:T(8,128)(2,1)} %param.15) | copy-start | bytes 2555908
  552.2 379.5 %copy-start.4 = (bf16[2,64,3328]{2,1,0:T(8,128)(2,1)S(1)}, bf16[2,64,3328]{2,1,0:T(8,128)(2,1)}, u32[]{:S(2)}) copy-start(bf16[2,64,3328]{2,1,0:T(8,128)(2,1)} %param.13) | copy-start | bytes 2555908
  552.2 379.5 %copy-start.5 = (bf16[2,64,3328]{2,1,0:T(8,128)(2,1)S(1)}, bf16[2,64,3328]{2,1,0:T(8,128)(2,1)}, u32[]{:S(2)}) copy-start(bf16[2,64,3328]{2,1,0:T(8,128)(2,1)} %param.14) | copy-start | bytes 2555908
  641.3 290.4 %copy-start.6 = (bf16[64,3328]{1,0:T(8,128)(2,1)S(1)}, bf16[64,3328]{1,0:T(8,128)(2,1)}, u32[]{:S(2)}) copy-start(bf16[64,3328]{1,0:T(8,128)(2,1)} %reduce-scatter.11.cloned.1.call-done) | copy-start | bytes 1277956
  722.2 209.6 %copy-start.7 = (bf16[64,3328]{1,0:T(8,128)(2,1)S(1)}, bf16[64,3328]{1,0:T(8,128)(2,1)}, u32[]{:S(2)}) copy-start(bf16[64,3328]{1,0:T(8,128)(2,1)} %reduce-scatter.13.cloned.1.call-done) | copy-start | bytes 1277956
  926.7 5.1 copy-start.8
  926.7 5.1 copy-start.9
  926.7 5.1 copy-start.10
  926.7 5.1 copy-start.11
  926.7 5.1 copy-start.12
  926.7 6.0 copy-start.13
Sparse Core Ops, SparseCore 0:
  10.8 46.3 all-gather.12
  60.0 43.4 all-gather.14
  106.3 43.5 all-gather.16
  152.5 43.4 all-gather.22
  198.7 43.4 all-gather.20
  245.0 43.5 all-gather.18
  399.5 76.8 reduce-scatter.14
  478.7 80.0 reduce-scatter.16
  561.1 80.2 reduce-scatter.10
  643.5 78.6 reduce-scatter.12
  724.5 80.6 reduce-scatter.6
  807.3 80.5 reduce-scatter.8
where the time goes:
time: 952 us; the launch traced here: 944 us
  waiting for transfers between devices  468 us (49%)
  matrix products  378 us (40%)
  blocking collectives  34 us (4%)
  other arithmetic  23.9 us (3%)
  local copies, waits for them, and re-layouts  22.8 us (2%)
  between operations  17.5 us (2%)
    reduce_scatter x6, waiting for transfers between devices, step(): lax.psum_scatter(by_w[name], 'dp', scatter_dimension=0, tiled=True)  331 us
    dot_general x5, matrix products, layer(): gate = jnp.dot(a, w['w_gate'], preferred_element_type=jnp.float32)  137 us
    all_gather x6, waiting for transfers between devices, fetched(): lax.all_gather(w[number], 'dp', axis=0, tiled=True)  135 us
    dot_general x5, matrix products, layer(): up = jnp.dot(a, w['w_up'], preferred_element_type=jnp.float32)  130 us
    dot_general x5, matrix products, matmul(): jnp.dot(a, w, preferred_element_type=jnp.float32).astype(jnp.bfloat16)  111 us
    psum x1, blocking collectives, step(): squares = lax.psum(sum((jnp.sum(g * g) for g in gradients)), 'dp')  34 us
  transfers between devices with their start and end apart: 12, of which 11 were waited for; matrix products, arithmetic and copies ran while one was open for 32% of the time, Pallas kernels for 0%

commit v1 on v0

v1 whole, which is shorter than its diff:
```python
import functools

import jax
import jax.numpy as jnp
from jax import lax
from jax.experimental import pallas as pl
from jax.experimental.pallas import tpu as pltpu
from jax.sharding import PartitionSpec as P

NAMES = ("w_gate", "w_up", "w_down")
BF, F32 = jnp.bfloat16, jnp.float32
ORDERS = ((0, 1, 2), (1, 2, 0), (2, 0, 1))
ANY = pl.BlockSpec(memory_space=pl.ANY)
VMEM = pl.BlockSpec(memory_space=pltpu.VMEM)


def spot():
    me = lax.axis_index("dp")
    return me, ((me // 8) % 2, (me // 4) % 2, (me // 2) % 2, me % 2)


def peer(axis):
    me, bits = spot()
    return {"dp": me + (1 - 2 * bits[axis]) * (8 >> axis)}


def greet():
    barrier = pltpu.get_barrier_semaphore()
    for axis in range(4):
        pl.semaphore_signal(barrier, inc=1, device_id=peer(axis), device_id_type=pl.DeviceIdType.MESH)
    pl.semaphore_wait(barrier, 4)


def thirds(columns, turn=0):
    tiles = columns // 128
    sizes = [tiles // 3 + (i < tiles % 3) for i in range(3)]
    parts, at = [], 0
    for i, size in enumerate(sizes):
        parts.append((pl.ds(at * 128, size * 128), size * 128, ORDERS[(i + turn) % 3]))
        at += size
    return parts


def send(src, dst, send_sem, recv_sem, axis):
    return pltpu.make_async_remote_copy(
        src_ref=src, dst_ref=dst, send_sem=send_sem, recv_sem=recv_sem, device_id=peer(axis), device_id_type=pl.DeviceIdType.MESH
    )


class Gather:
    scratch = [pltpu.SemaphoreType.DMA((3, 3, 2)), pltpu.SemaphoreType.DMA((2,)), pltpu.SemaphoreType.DMA]

    def __init__(self, own, whole, sems, turn=0):
        self.own, self.whole, (self.sems, self.side, self.local) = own, whole, sems
        self.parts = thirds(own.shape[-1], turn)
        _, self.bits = spot()

    def at(self, cols, done, flip=None):
        index = [slice(None) if a in done else self.bits[a] for a in range(4)]
        if flip is not None:
            index[flip] = 1 - self.bits[flip]
        return self.whole.at[(*index, slice(None), cols)]

    def place(self):
        return pltpu.make_async_copy(self.own, self.at(slice(None), ()), self.local)

    def hop(self, p, phase):
        cols, _, order = self.parts[p]
        here = self.at(cols, order[:phase])
        return send(self.own.at[:, cols] if phase == 0 else here, here, self.sems.at[p, phase, 0], self.sems.at[p, phase, 1], order[phase])

    def across(self, src):
        return lambda dst: send(src, dst, self.side.at[0], self.side.at[1], 3)

    def stages(self):
        def begin():
            self.place().start()
            for p in range(3):
                self.hop(p, 0).start()
            self.across(self.own)(self.at(slice(None), ())).start()

        def go_on(phase):
            def run():
                if phase == 1:
                    self.place().wait()
                for p, (cols, _, order) in enumerate(self.parts):
                    self.hop(p, phase - 1).wait()
                    if phase < 3:
                        self.hop(p, phase).start()
                    got = self.at(cols, order[: phase - 1], order[phase - 1])
                    self.across(got)(got).start()

            return run

        def end():
            half = self.at(slice(None), (0, 1, 2))
            self.across(half)(half).wait()

        return [begin, go_on(1), go_on(2), go_on(3), end]


class Scatter:
    @staticmethod
    def scratch(rows, columns):
        return [
            pltpu.VMEM((2, 2, 2, rows, columns), BF),
            pltpu.VMEM((2, 2, 2, rows, columns), BF),
            pltpu.VMEM((4, rows, columns), BF),
            pltpu.VMEM((2, rows, columns), BF),
            pltpu.VMEM((1, rows, columns), BF),
            pltpu.SemaphoreType.DMA((3, 4, 2)),
            pltpu.SemaphoreType.DMA,
        ]

    def __init__(self, whole, mine, scratch, turn=0):
        self.whole, self.mine = whole, mine
        self.own, *self.got, self.sems, self.local = scratch
        self.parts = thirds(whole.shape[-1], turn)
        _, self.bits = spot()

    def index(self, done, flip=None):
        index = [self.bits[a] if a in done else slice(None) for a in range(3)]
        if flip is not None:
            index[flip] = 1 - self.bits[flip]
        return tuple(index)

    def load(self):
        return pltpu.make_async_copy(self.whole.at[:, :, :, self.bits[3]], self.own, self.local)

    def first(self, p):
        cols = self.parts[p][0]
        return send(
            self.whole.at[:, :, :, 1 - self.bits[3], :, cols],
            self.got[0].at[:, :, :, :, cols],
            self.sems.at[p, 0, 0],
            self.sems.at[p, 0, 1],
            3,
        )

    def blocks(self, p, phase):
        order = self.parts[p][2]
        free = order[phase:]
        for k in range(2 ** len(free)):
            index = [self.bits[a] for a in range(3)]
            index[order[phase - 1]] = 1 - self.bits[order[phase - 1]]
            for i, a in enumerate(free):
                index[a] = (k >> (len(free) - 1 - i)) & 1
            yield tuple(index), k

    def hops(self, p, phase):
        cols = self.parts[p][0]
        order = self.parts[p][2]
        for index, k in self.blocks(p, phase):
            yield send(
                self.own.at[(*index, slice(None), cols)],
                self.got[phase].at[k, :, cols],
                self.sems.at[p, phase, 0],
                self.sems.at[p, phase, 1],
                order[phase - 1],
            )

    def landed(self, p, phase):
        cols = self.parts[p][0]
        whole = self.got[phase].at[:, :, cols]
        return send(whole, whole, self.sems.at[p, phase, 0], self.sems.at[p, phase, 1], self.parts[p][2][phase - 1])

    def total(self, p, index, upto):
        cols, _, order = self.parts[p]
        value = self.own[(*index, slice(None), cols)].astype(F32) + self.got[0][(*index, slice(None), cols)].astype(F32)
        for phase in range(1, upto):
            place = 0
            for a in order[phase:]:
                place = 2 * place + index[a]
            value += self.got[phase][place, :, cols].astype(F32)
        return value

    def stages(self):
        def begin():
            self.load().start()
            for p in range(3):
                self.first(p).start()

        def add(phase):
            def run():
                if phase == 1:
                    self.load().wait()
                for p, (cols, _, _) in enumerate(self.parts):
                    if phase == 1:
                        self.first(p).wait()
                    else:
                        self.landed(p, phase - 1).wait()
                    for index, _ in self.blocks(p, phase):
                        self.own[(*index, slice(None), cols)] = self.total(p, index, phase).astype(BF)
                    for hop in self.hops(p, phase):
                        hop.start()

            return run

        def end():
            for p, (cols, _, _) in enumerate(self.parts):
                self.landed(p, 3).wait()
                self.mine[:, cols] = self.total(p, self.bits[:3], 4).astype(BF)

        return [begin, add(1), add(2), add(3), end]


def interleave(jobs, lag=1):
    lists = [job.stages() for job in jobs]
    for t in range(max(len(s) + lag * j for j, s in enumerate(lists))):
        for j, s in reversed(list(enumerate(lists))):
            if 0 <= t - lag * j < len(s):
                s[t - lag * j]()


def chunked(refs, sizes):
    out, at = [], 0
    for size in sizes:
        out.append(refs[at : at + size])
        at += size
    return out


def gather_all(weights, identity):
    layers, n = weights[0].shape[0], len(weights)

    def kernel(*refs):
        own, whole, scratch = refs[:n], refs[n : n + n * layers], refs[n + n * layers :]
        greet()
        scratch = chunked(scratch, [3] * (n * layers))
        interleave([Gather(own[i % n].at[i // n], whole[i], scratch[i], i) for i in range(n * layers)])

    out = pl.pallas_call(
        kernel,
        in_specs=[VMEM] * n,
        out_specs=[ANY] * (n * layers),
        out_shape=[jax.ShapeDtypeStruct((2, 2, 2, 2, *w.shape[1:]), BF) for _ in range(layers) for w in weights],
        scratch_shapes=Gather.scratch * (n * layers),
        compiler_params=pltpu.CompilerParams(collective_id=identity, has_side_effects=True, vmem_limit_bytes=60 << 20),
    )(*weights)
    out = [w.reshape(16 * w.shape[4], w.shape[5]) for w in out]
    return [dict(zip(NAMES, out[n * i : n * i + n])) for i in range(layers)]


def scatter_all(terms, identity):
    n = len(terms)
    terms = [t.reshape(2, 2, 2, 2, t.shape[0] // 16, t.shape[1]) for t in terms]

    def kernel(*refs):
        whole, mine, scratch = refs[:n], refs[n : 2 * n], refs[2 * n :]
        greet()
        scratch = chunked(scratch, [7] * n)
        interleave([Scatter(whole[i], mine[i], scratch[i], i) for i in range(n)])

    return pl.pallas_call(
        kernel,
        in_specs=[ANY] * n,
        out_specs=[VMEM] * n,
        out_shape=[jax.ShapeDtypeStruct(t.shape[4:], BF) for t in terms],
        scratch_shapes=[s for t in terms for s in Scatter.scratch(*t.shape[4:])],
        compiler_params=pltpu.CompilerParams(collective_id=identity, has_side_effects=True, vmem_limit_bytes=60 << 20),
    )(*terms)


def sum_of_squares(gradients, identity):
    n = len(gradients)

    def kernel(*refs):
        ours, out, term, slots, sems = refs[:n], *refs[n:]
        me, _ = spot()
        barrier = pltpu.get_barrier_semaphore()
        for k in range(1, 16):
            pl.semaphore_signal(barrier, inc=1, device_id={"dp": (me + k) % 16}, device_id_type=pl.DeviceIdType.MESH)
        pl.semaphore_wait(barrier, 15)
        total = jnp.zeros((8, 128), F32)
        for g in ours:
            rows, columns = g.shape

            def add(i, total, g=g, columns=columns):
                wide = g[pl.ds(pl.multiple_of(i * 16, 16), 16), :].astype(F32)
                wide = wide * wide
                for j in range(columns // 128):
                    total = total + wide[:8, 128 * j : 128 * j + 128] + wide[8:, 128 * j : 128 * j + 128]
                return total

            total = lax.fori_loop(0, rows // 16, add, total)
        term[...] = total
        copies = [
            pltpu.make_async_remote_copy(
                src_ref=term,
                dst_ref=slots.at[k - 1],
                send_sem=sems.at[k - 1, 0],
                recv_sem=sems.at[k - 1, 1],
                device_id={"dp": (me + k) % 16},
                device_id_type=pl.DeviceIdType.MESH,
            )
            for k in range(1, 16)
        ]
        for copy in copies:
            copy.start()
        for copy in copies:
            copy.wait()
        total = term[...]
        for k in range(15):
            total = total + slots[k]
        out[...] = total

    return pl.pallas_call(
        kernel,
        in_specs=[VMEM] * n,
        out_specs=VMEM,
        out_shape=jax.ShapeDtypeStruct((8, 128), F32),
        scratch_shapes=[pltpu.VMEM((8, 128), F32), pltpu.VMEM((15, 8, 128), F32), pltpu.SemaphoreType.DMA((15, 2))],
        compiler_params=pltpu.CompilerParams(collective_id=identity, has_side_effects=True),
    )(*gradients)


def matmul(a, w):
    return jnp.dot(a, w, preferred_element_type=F32).astype(BF)


def normed(h):
    wide = h.astype(F32)
    scale = lax.rsqrt(jnp.mean(wide**2, -1, keepdims=True) + 1e-6)
    return (wide * scale).astype(BF)


def layer(h, w):
    a = normed(h)
    gate = jnp.dot(a, w["w_gate"], preferred_element_type=F32)
    up = jnp.dot(a, w["w_up"], preferred_element_type=F32)
    return h + matmul((jax.nn.silu(gate) * up).astype(BF), w["w_down"])


def adamw(w, m, v, g):
    m = 0.9 * m + 0.1 * g
    v = 0.95 * v + 0.05 * g * g
    step = m * lax.rsqrt(v + 1e-8) + 0.1 * w
    return (w - 0.02 * step).astype(BF), m, v


def solution(mesh):
    def step(x, dy, *arrays):
        weights, m, v = (arrays[i : i + 3] for i in (0, 3, 6))
        layers = weights[0].shape[0]
        whole = gather_all(weights, 0)
        h, kept = x[0], []
        for number in range(layers):
            kept.append(h)
            h = layer(h, whole[number])
        by_h, mine = dy[0], [None] * layers
        for number in reversed(range(layers)):
            _, back = jax.vjp(lambda w, h: layer(h, w), whole[number], kept[number])
            by_w, by_h = back(by_h)
            mine[number] = scatter_all([by_w[name] for name in NAMES], 1 + number)
        squares = jnp.sum(sum_of_squares([g for one in mine for g in one], 1 + layers))
        gradients = [jnp.stack([mine[number][i] for number in range(layers)]).astype(F32) for i in range(3)]
        factor = jnp.minimum(1.0, 0.5 * lax.rsqrt(squares / (16 * sum(g.size for g in gradients)) + 1e-30))
        new = [adamw(w.astype(F32), m, v, g * factor) for w, m, v, g in zip(weights, m, v, gradients, strict=True)]
        return tuple(one[which] for which in range(3) for one in new)

    states, cut = P(("rep", "dp"), None, None), P(None, "dp", None)
    return jax.shard_map(
        step,
        mesh=mesh,
        in_specs=(states, states) + (cut,) * 9,
        out_specs=(P("rep", "dp", None),) * 9,
        check_vma=False,
    )
```

time: 952 us -> 720 us (0.76)
  waiting for transfers between devices: 468 us -> 0 us
  Pallas kernels: 0 us -> 301 us
  blocking collectives: 34 us -> 0 us
  between operations: 17.5 us -> 2.1 us
  local copies, waits for them, and re-layouts: 22.8 us -> 13.1 us
    reduce_scatter x6 -> x0, waiting for transfers between devices: 331 us -> none  [step(): lax.psum_scatter(by_w[name], 'dp', scatter_dimension=0, tiled=True)]
    pallas_call x0 -> x4, Pallas kernels: none -> 301 us  [the longest x2 151 us: scatter_all(): pl.pallas_call(kernel, in_specs=[ANY] * n, out_specs=[VMEM] * n, out_shap...]
    all_gather x6 -> x0, waiting for transfers between devices: 135 us -> none  [fetched(): lax.all_gather(w[number], 'dp', axis=0, tiled=True)]
    psum x1 -> x0, blocking collectives: 34 us -> none  [step(): squares = lax.psum(sum((jnp.sum(g * g) for g in gradients)), 'dp')]
  transfers between devices with their start and end apart: 12 -> 0, of which waited for: 11 -> 0; matrix products, arithmetic and copies ran while one was open for 32% -> 0% of each run, Pallas kernels for 0% -> 0%
where the time goes in v1:
time: 720 us; the launch traced here: 712 us
  matrix products  374 us (52%)
  Pallas kernels  301 us (42%)
  other arithmetic  21.3 us (3%)
  local copies, waits for them, and re-layouts  13.1 us (2%)
    pallas_call x2, Pallas kernels, scatter_all(): pl.pallas_call(kernel, in_specs=[ANY] * n, out_specs=[VMEM] * n, out_shap...  151 us
    pallas_call x1, Pallas kernels, gather_all(): pl.pallas_call(kernel, in_specs=[VMEM] * n, out_specs=[ANY] * (n * layers...  141 us
    dot_general x5, matrix products, layer(): gate = jnp.dot(a, w['w_gate'], preferred_element_type=F32)  135 us
    dot_general x5, matrix products, layer(): up = jnp.dot(a, w['w_up'], preferred_element_type=F32)  128 us
    dot_general x5, matrix products, matmul(): return jnp.dot(a, w, preferred_element_type=F32).astype(BF)  112 us

profile of v1, /device:TPU:0, one launch (start us, length us, event | category | flops | bytes accessed | tf_op | source)
XLA Modules:
  0.0 712.3 jit_solution(12121923029269560219)
XLA Ops:
  0.6 141.2 %shard_map.178 = (bf16[2,2,2,2,64,3328]{5,4,3,2,1,0:T(8,128)(2,1)}, bf16[2,2,2,2,64,3328]{5,4,3,2,1,0:T(8,128)(2,1)}, bf16[2,2,2,2,208,1024]{5,4,3,2,1,0:T(8,128...) custom-call(bf16[2,64,3328]{2,1,0:T(8,128)(2,1)} %refs_0_.1, ...), custom_call_target="tpu_custom_call" | custom-call | tf_op jit(solution)/shard_map/pallas_call | solution.py:232
  141.8 6.5 copy.20
  148.4 3.1 fusion.15
  151.4 22.0 %fusion.43 = f32[2048,3328]{1,0:T(8,128)} fusion(bf16[1024,3328]{1,0:T(8,128)(2,1)} %bitcast.82, bf16[1,2048,1024]{2,1,0:T(8,128)(2,1)} %param.11, f32[2048]{0:T(1024)S(1)} %add_rsqrt_fusion), kind=kOutput, calls=%fused_computation.65 | convolution fusion | flops 13964935168 | bytes 38281216 | tf_op jit(solution)/shard_map/dot_general | solution.py:329
  173.5 32.7 %multiply_convert_fusion.1 = (bf16[2048,3328]{1,0:T(8,128)(2,1)}, f32[2048,3328]{1,0:T(8,128)}) fusion(f32[2048,3328]{1,0:T(8,128)} %fusion.43, bf16[1024,3328]{1,0:T(8,128)(2,1)} %bitcast.81, bf16[1,2048,1024]{2,1,0:T(8,128)(2,1)} %param.11, f32[2048]{0:T(1024)S(1)} %add_rsqrt_fusion), kind=kOutput, calls=%fused_computation.17 | convolution fusion | flops 14005829632 | bytes 79175680 | tf_op jit(solution)/shard_map/dot_general | solution.py:330
  206.2 22.3 %fusion.19 = (f32[2048]{0:T(1024)S(1)}, bf16[2048,1024]{0,1:T(8,128)(2,1)}) fusion(bf16[2048,3328]{1,0:T(8,128)(2,1)} %get-tuple-element.42, bf16[3328,1024]{1,0:T(8,128)(2,1)} %bitcast.74, bf16[1,2048,1024]{1,2,0:T(8,128)(2,1)} %copy.20), kind=kOutput, calls=%fused_computation.37 | convolution fusion | flops 13969127424 | bytes 28844032 | tf_op jit(solution)/shard_map/dot_general | solution.py:318
  228.5 21.4 %convolution_convert_fusion.1 = bf16[3328,2048]{0,1:T(8,128)(2,1)} fusion(bf16[3328,1024]{1,0:T(8,128)(2,1)} %bitcast.80, bf16[1,2048,1024]{2,1,0:T(8,128)(2,1)} %param.12), kind=kOutput, calls=%fused_computation.23 | convolution fusion | flops 13965459456 | bytes 24641536 | tf_op jit(solution)/shard_map/transpose(jvp())/dot_general | solution.py:318
  250.0 0.0 copy-start.13
  250.0 21.0 %fusion.37 = f32[2048,3328]{1,0:T(8,128)} fusion(bf16[1024,3328]{1,0:T(8,128)(2,1)} %bitcast.78, bf16[2048,1024]{0,1:T(8,128)(2,1)S(1)} %copy-done, f32[2048]{0:T(1024)S(1)} %fusion.57), kind=kOutput, calls=%fused_computation.53 | convolution fusion | flops 13964935168 | bytes 38281216 | tf_op jit(solution)/shard_map/jvp()/dot_general | solution.py:330
  271.0 39.8 %fusion.2 = (bf16[2048,3328]{1,0:T(8,128)(2,1)}, f32[2048,3328]{1,0:T(8,128)}) fusion(f32[2048,3328]{1,0:T(8,128)} %fusion.37, bf16[3328,2048]{0,1:T(8,128)(2,1)} %convolution_convert_fusion.1, bf16[1024,3328]{1,0:T(8,128)(2,1)} %bitcast.76, bf16[2048,1024]{0,1:T(8,128)(2,1)} %get-tuple-element.45, f32[2048]{0:T(1024)S(1)} %fusion.57), kind=kOutput, calls=%fused_computation.6 | convolution fusion | flops 14046724096 | bytes 92807168 | tf_op jit(solution)/shard_map/jvp()/dot_general | solution.py:329
  310.8 24.0 %fusion.12 = bf16[2048,1024]{0,1:T(8,128)(2,1)} fusion(bf16[1024,3328]{1,0:T(8,128)(2,1)} %bitcast.79, bf16[3328,2048]{0,1:T(8,128)(2,1)} %convolution_convert_fusion.1, f32[2048,3328]{1,0:T(8,128)} %get-tuple-element.47), kind=kOutput, calls=%fused_computation.21 | convolution fusion | flops 13999538176 | bytes 51904512 | tf_op jit(solution)/shard_map/transpose(jvp())/dot_general | solution.py:330
  334.8 19.9 %fusion.21 = (f32[2048]{0:T(1024)S(1)}, bf16[2048,1024]{0,1:T(8,128)(2,1)}) fusion(bf16[2048,1024]{0,1:T(8,128)(2,1)S(1)} %copy-done.1, bf16[2048,1024]{0,1:T(8,128)(2,1)} %fusion.12, bf16[2048,3328]{1,0:T(8,128)(2,1)} %get-tuple-element.46, bf16[1024,3328]{1,0:T(8,128)(2,1)S(1)} %bitcast.77), kind=kOutput, calls=%fused_computation.39 | convolution fusion | flops 13969127424 | bytes 33038336 | tf_op jit(solution)/shard_map/transpose(jvp())/dot_general | solution.py:329
  354.7 6.5 copy.21
  361.3 7.6 %fusion.30 = bf16[2048,1024]{0,1:T(8,128)(2,1)} fusion(bf16[2048,1024]{0,1:T(8,128)(2,1)} %get-tuple-element.45, bf16[2048,1024]{0,1:T(8,128)(2,1)} %get-tuple-element.49, bf16[1,2048,1024]{1,2,0:T(8,128)(2,1)} %copy.21, f32[2048]{0:T(1024)S(1)} %multiply_multiply_fusion.3, f32[2048]{0:T(1024)S(1)} %fusion.57), kind=kLoop, calls=%fused_computation.48 | loop fusion | flops 14680064 | bytes 16793600 | tf_op jit(solution)/shard_map/transpose(jvp())/add_any | solution.py:322
  368.9 21.3 %convolution_convert_fusion = bf16[2048,3328]{1,0:T(8,128)(2,1)} fusion(bf16[2048,1024]{0,1:T(8,128)(2,1)} %fusion.30, bf16[3328,1024]{1,0:T(8,128)(2,1)} %bitcast.75), kind=kOutput, calls=%fused_computation.22 | convolution fusion | flops 13965459456 | bytes 24641536 | tf_op jit(solution)/shard_map/transpose(jvp())/dot_general | solution.py:318
  390.2 31.5 %fusion.22 = bf16[1024,3328]{1,0:T(8,128)(2,1)} fusion(f32[2048,3328]{1,0:T(8,128)} %fusion.43, f32[2048,3328]{1,0:T(8,128)} %get-tuple-element.43, bf16[2048,3328]{1,0:T(8,128)(2,1)} %convolution_convert_fusion, bf16[1,2048,1024]{1,2,0:T(8,128)(2,1)} %copy.20, f32[2048]{0:T(1024)S(1)} %copy-done.18), kind=kOutput, calls=%fused_computation.41 | convolution fusion | flops 14043316224 | bytes 79175680 | tf_op jit(solution)/shard_map/transpose(jvp())/dot_general | solution.py:329
  421.7 25.5 %fusion.27 = bf16[1024,3328]{1,0:T(8,128)(2,1)} fusion(bf16[2048,3328]{1,0:T(8,128)(2,1)} %convolution_convert_fusion, f32[2048,3328]{1,0:T(8,128)} %fusion.43, bf16[1,2048,1024]{1,2,0:T(8,128)(2,1)} %copy.20, f32[2048]{0:T(1024)S(1)} %copy-done.18), kind=kOutput, calls=%fused_computation.44 | convolution fusion | flops 14009237504 | bytes 51912704 | tf_op jit(solution)/shard_map/transpose(jvp())/dot_general | solution.py:330
  447.1 19.9 %convolution_convert_fusion.3 = bf16[3328,1024]{1,0:T(8,128)(2,1)} fusion(bf16[2048,3328]{1,0:T(8,128)(2,1)} %get-tuple-element.42, bf16[2048,1024]{0,1:T(8,128)(2,1)S(1)} %copy-done.3), kind=kOutput, calls=%fused_computation.46 | convolution fusion | flops 13962051584 | bytes 24641536 | tf_op jit(solution)/shard_map/transpose(jvp())/dot_general | solution.py:318
  467.0 0.0 copy-start.14
  467.0 75.6 %shard_map.179 = (bf16[64,3328]{1,0:T(8,128)(2,1)}, bf16[64,3328]{1,0:T(8,128)(2,1)}, bf16[208,1024]{1,0:T(8,128)(2,1)}) custom-call(bf16[2,2,2,2,64,3328]{5,4,3,2,1,0:T(8,128)(2,1)} %bitcast.62, bf16[2,2,2,2,64,3328]{5,4,3,2,1,0:T(8,128)(2,1)} %bitcast.63, bf16[2,2,2,2,208,1024]{5,4,3,2,1,0:T(8,128)(2,1)} %bitcast.66), custom_call_target="tpu_custom_call" | custom-call | tf_op jit(solution)/shard_map/pallas_call | solution.py:254
  542.6 21.4 %convolution_convert_fusion.2 = bf16[1024,3328]{1,0:T(8,128)(2,1)} fusion(bf16[2048,3328]{1,0:T(8,128)(2,1)} %get-tuple-element.46, bf16[2048,1024]{0,1:T(8,128)(2,1)} %get-tuple-element.45, f32[2048]{0:T(1024)S(1)} %copy-done.14), kind=kOutput, calls=%fused_computation.45 | convolution fusion | flops 13964935168 | bytes 24649728 | tf_op jit(solution)/shard_map/transpose(jvp())/dot_general | solution.py:329
  564.0 24.4 %fusion.26 = bf16[1024,3328]{1,0:T(8,128)(2,1)} fusion(bf16[3328,2048]{0,1:T(8,128)(2,1)} %convolution_convert_fusion.1, bf16[2048,1024]{0,1:T(8,128)(2,1)S(1)} %copy-done.2, f32[2048]{0:T(1024)S(1)} %copy-done.14, f32[2048,3328]{1,0:T(8,128)} %get-tuple-element.47), kind=kOutput, calls=%fused_computation.43 | convolution fusion | flops 14009237504 | bytes 51912704 | tf_op jit(solution)/shard_map/transpose(jvp())/dot_general | solution.py:330
  588.4 27.3 %fusion.25 = bf16[3328,1024]{1,0:T(8,128)(2,1)} fusion(f32[2048,3328]{1,0:T(8,128)} %fusion.37, bf16[1,2048,1024]{2,1,0:T(8,128)(2,1)} %param.12, f32[2048,3328]{1,0:T(8,128)} %get-tuple-element.47), kind=kOutput, calls=%fused_computation.42 | convolution fusion | flops 14002946048 | bytes 65536000 | tf_op jit(solution)/shard_map/transpose(jvp())/dot_general | solution.py:318
  615.7 0.0 copy-start.5
  615.7 0.0 copy-start.6
  615.8 75.2 %shard_map.180 = (bf16[64,3328]{1,0:T(8,128)(2,1)}, bf16[64,3328]{1,0:T(8,128)(2,1)}, bf16[208,1024]{1,0:T(8,128)(2,1)}) custom-call(bf16[2,2,2,2,64,3328]{5,4,3,2,1,0:T(8,128)(2,1)} %bitcast.64, bf16[2,2,2,2,64,3328]{5,4,3,2,1,0:T(8,128)(2,1)} %bitcast.65, bf16[2,2,2,2,208,1024]{5,4,3,2,1,0:T(8,128)(2,1)} %bitcast.67), custom_call_target="tpu_custom_call" | custom-call | tf_op jit(solution)/shard_map/pallas_call | solution.py:254
  690.9 9.4 %shard_map.181 = f32[8,128]{1,0:T(8,128)} custom-call(bf16[64,3328]{1,0:T(8,128)(2,1)} %get-tuple-element.27.refs_0_, bf16[64,3328]{1,0:T(8,128)(2,1)} %get-tuple-element.29.refs_1_, bf16[208,1024]{1,0:T(8,128)(2,1)} %get-tuple-element.30.refs_2_, bf16[64,3328]{1,0:T(8,128)(2,1)} %get-tuple-element.28.refs_3_, bf16[64,3328]{1,0:T(8,128)(2,1)} %get-tuple-element.31.refs_4_, ...), custom_call_target="tpu_custom_call" | custom-call | tf_op jit(solution)/shard_map/pallas_call | solution.py:307
  700.4 1.3 reduce_sum.41
  702.4 0.0 copy-start.4
  702.4 0.0 copy-start.7
  702.5 6.6 fusion.47
  709.1 2.7 fusion.53
  (37 shorter events, 0.1 us)
Async XLA Ops:
  151.4 22.1 %copy-start.17 = (f32[2048]{0:T(1024)}, f32[2048]{0:T(1024)S(1)}, u32[]{:S(2)}) copy-start(f32[2048]{0:T(1024)S(1)} %add_rsqrt_fusion) | copy-start | bytes 24580
  228.5 21.5 %copy-start.15 = (f32[2048]{0:T(1024)}, f32[2048]{0:T(1024)S(1)}, u32[]{:S(2)}) copy-start(f32[2048]{0:T(1024)S(1)} %get-tuple-element.44) | copy-start | bytes 24580
  228.5 21.5 %copy-start = (bf16[2048,1024]{0,1:T(8,128)(2,1)S(1)}, bf16[2048,1024]{0,1:T(8,128)(2,1)}, u32[]{:S(2)}) copy-start(bf16[2048,1024]{0,1:T(8,128)(2,1)} %get-tuple-element.45) | copy-start | bytes 12582916
  250.0 111.3 %copy-start.13 = (f32[2048]{0:T(1024)}, f32[2048]{0:T(1024)S(1)}, u32[]{:S(2)}) copy-start(f32[2048]{0:T(1024)S(1)} %fusion.57) | copy-start | bytes 24580
  310.8 24.0 %copy-start.1 = (bf16[2048,1024]{0,1:T(8,128)(2,1)S(1)}, bf16[2048,1024]{0,1:T(8,128)(2,1)}, u32[]{:S(2)}) copy-start(bf16[2048,1024]{0,1:T(8,128)(2,1)} %get-tuple-element.45) | copy-start | bytes 12582916
  310.8 24.0 %copy-start.19 = (bf16[2,2,2,2,64,3328]{5,4,3,2,1,0:T(8,128)(2,1)S(1)}, bf16[2,2,2,2,64,3328]{5,4,3,2,1,0:T(8,128)(2,1)}, u32[]{:S(2)}) copy-start(bf16[2,2,2,2,64,3328]{5,4,3,2,1,0:T(8,128)(2,1)} %get-tuple-element.24) | copy-start | bytes 20447236
  354.7 6.5 copy-start.16
  368.9 21.3 %copy-start.18 = (f32[2048]{0:T(1024)S(1)}, f32[2048]{0:T(1024)}, u32[]{:S(2)}) copy-start(f32[2048]{0:T(1024)} %copy-done.17) | copy-start | bytes 24580
  421.7 25.5 %copy-start.3 = (bf16[2048,1024]{0,1:T(8,128)(2,1)S(1)}, bf16[2048,1024]{0,1:T(8,128)(2,1)}, u32[]{:S(2)}) copy-start(bf16[2048,1024]{0,1:T(8,128)(2,1)} %fusion.30) | copy-start | bytes 12582916
  467.0 75.6 %copy-start.14 = (f32[2048]{0:T(1024)S(1)}, f32[2048]{0:T(1024)}, u32[]{:S(2)}) copy-start(f32[2048]{0:T(1024)} %copy-done.13) | copy-start | bytes 24580
  542.6 21.4 %copy-start.2 = (bf16[2048,1024]{0,1:T(8,128)(2,1)S(1)}, bf16[2048,1024]{0,1:T(8,128)(2,1)}, u32[]{:S(2)}) copy-start(bf16[2048,1024]{0,1:T(8,128)(2,1)} %get-tuple-element.45) | copy-start | bytes 12582916
  615.7 86.6 %copy-start.5 = (bf16[2,64,3328]{2,1,0:T(8,128)(2,1)S(1)}, bf16[2,64,3328]{2,1,0:T(8,128)(2,1)}, u32[]{:S(2)}) copy-start(bf16[2,64,3328]{2,1,0:T(8,128)(2,1)} %refs_0_.1) | copy-start | bytes 2555908
  615.7 86.6 %copy-start.6 = (bf16[2,64,3328]{2,1,0:T(8,128)(2,1)S(1)}, bf16[2,64,3328]{2,1,0:T(8,128)(2,1)}, u32[]{:S(2)}) copy-start(bf16[2,64,3328]{2,1,0:T(8,128)(2,1)} %refs_1_.1) | copy-start | bytes 2555908
  615.7 86.6 %copy-start.10 = (bf16[64,3328]{1,0:T(8,128)(2,1)S(1)}, bf16[64,3328]{1,0:T(8,128)(2,1)}, u32[]{:S(2)}) copy-start(bf16[64,3328]{1,0:T(8,128)(2,1)} %get-tuple-element.27.refs_0_) | copy-start | bytes 1277956
  615.8 86.6 %copy-start.11 = (bf16[64,3328]{1,0:T(8,128)(2,1)S(1)}, bf16[64,3328]{1,0:T(8,128)(2,1)}, u32[]{:S(2)}) copy-start(bf16[64,3328]{1,0:T(8,128)(2,1)} %get-tuple-element.29.refs_1_) | copy-start | bytes 1277956
  702.4 6.7 copy-start.4
  702.4 6.7 copy-start.7
  702.4 6.6 copy-start.8
  702.4 6.6 copy-start.9
  702.4 6.6 copy-start.12

commit v2 on v1

--- a/solution.py
+++ b/solution.py
@@ -220,25 +220,281 @@
     return out
 
 
-def gather_all(weights, identity):
-    layers, n = weights[0].shape[0], len(weights)
+def normed(h):
+    wide = h.astype(F32)
+    scale = lax.rsqrt(jnp.mean(wide**2, -1, keepdims=True) + 1e-6)
+    return (wide * scale).astype(BF)
+
+
+def dot(a, b, over=(1, 0)):
+    return lax.dot_general(a, b, (((over[0],), (over[1],)), ((), ())), preferred_element_type=F32)
+
+
+class Gathers:
+    def __init__(self, own, picks):
+        self.args, self.picks = list(own), picks
+        self.in_specs = [VMEM] * len(own)
+        self.out_shape = [jax.ShapeDtypeStruct((2, 2, 2, 2, *own[i].shape[1:]), BF) for i, _ in picks]
+        self.out_specs = [ANY] * len(picks)
+        self.scratch = Gather.scratch * len(picks)
+
+    def jobs(self, ins, outs, scratch):
+        scratch = chunked(scratch, [3] * len(self.picks))
+        return [Gather(ins[i].at[number], outs[n], scratch[n], n) for n, (i, number) in enumerate(self.picks)]
+
+    @staticmethod
+    def finished(outs):
+        return [w.reshape(16 * w.shape[4], w.shape[5]) for w in outs]
+
+
+class Scatters:
+    def __init__(self, terms):
+        self.args = [t.reshape(2, 2, 2, 2, t.shape[0] // 16, t.shape[1]) for t in terms]
+        self.in_specs = [ANY] * len(terms)
+        self.out_shape = [jax.ShapeDtypeStruct(t.shape[4:], BF) for t in self.args]
+        self.out_specs = [VMEM] * len(terms)
+        self.scratch = [s for t in self.args for s in Scatter.scratch(*t.shape[4:])]
+
+    def jobs(self, ins, outs, scratch):
+        scratch = chunked(scratch, [7] * len(self.args))
+        return [Scatter(ins[n], outs[n], scratch[n], n) for n in range(len(self.args))]
+
+    @staticmethod
+    def finished(outs):
+        return list(outs)
+
+
+class Nothing:
+    args, in_specs, out_shape, out_specs, scratch = [], [], [], [], []
+
+    @staticmethod
+    def finished(outs):
+        return []
+
+
+def call(name, identity, steps, body, args, in_specs, out_shape, out_specs, scratch, traffic, times):
+    counts = [len(args), len(traffic.args), len(out_shape), len(traffic.out_shape), len(scratch), len(traffic.scratch)]
 
     def kernel(*refs):
-        own, whole, scratch = refs[:n], refs[n : n + n * layers], refs[n + n * layers :]
-        greet()
-        scratch = chunked(scratch, [3] * (n * layers))
-        interleave([Gather(own[i % n].at[i // n], whole[i], scratch[i], i) for i in range(n * layers)])
-
+        ins, t_ins, outs, t_outs, own, t_scratch = chunked(refs, counts)
+        step = pl.program_id(0)
+        plan = []
+        if traffic.args:
+            for n, (job, when) in enumerate(zip(traffic.jobs(t_ins, t_outs, t_scratch), times, strict=True)):
+                plan += [(at, -n, stage) for at, stage in zip(when, job.stages(), strict=True)]
+            plan.sort(key=lambda one: one[:2])
+
+        def run(at, first=False):
+            now = [stage for when, _, stage in plan if (when == at if at < steps else when >= steps)]
+            if now or first:
+
+                @pl.when(step == min(at, steps - 1))
+                def _():
+                    if first and plan:
+                        greet()
+                    for stage in now:
+                        stage()
+
+        for at in range(steps):
+            run(at, at == 0)
+        body(step, ins, outs, own)
+        run(steps)
+
+    params = dict(vmem_limit_bytes=62 << 20, dimension_semantics=("arbitrary",))
+    if traffic.args:
+        params |= dict(collective_id=identity, has_side_effects=True)
     out = pl.pallas_call(
         kernel,
-        in_specs=[VMEM] * n,
-        out_specs=[ANY] * (n * layers),
-        out_shape=[jax.ShapeDtypeStruct((2, 2, 2, 2, *w.shape[1:]), BF) for _ in range(layers) for w in weights],
-        scratch_shapes=Gather.scratch * (n * layers),
-        compiler_params=pltpu.CompilerParams(collective_id=identity, has_side_effects=True, vmem_limit_bytes=60 << 20),
-    )(*weights)
-    out = [w.reshape(16 * w.shape[4], w.shape[5]) for w in out]
-    return [dict(zip(NAMES, out[n * i : n * i + n])) for i in range(layers)]
+        name=name,
+        grid=(steps,),
+        in_specs=in_specs + traffic.in_specs,
+        out_specs=out_specs + traffic.out_specs,
+        out_shape=out_shape + traffic.out_shape,
+        scratch_shapes=scratch + traffic.scratch,
+        compiler_params=pltpu.CompilerParams(**params),
+    )(*args, *traffic.args)
+    return (*out[: len(out_shape)], traffic.finished(out[len(out_shape) :]))
+
+
+def fixed(shape):
+    return pl.BlockSpec(shape, lambda i: (0,) * len(shape), pipeline_mode=pl.Buffered(1))
+
+
+def down(shape):
+    return pl.BlockSpec(shape, lambda i: (i, 0))
+
+
+def along(shape):
+    return pl.BlockSpec(shape, lambda i: (0, i))
+
+
+def like(shape, dtype=BF):
+    return jax.ShapeDtypeStruct(shape, dtype)
+
+
+WIDE = 256
+TALL = 256
+
+
+def start(x, identity, traffic, times):
+    tokens, d = x.shape
+    rows = tokens // 8
+
+    def body(step, ins, outs, _):
+        outs[0][...] = normed(ins[0][...])
+
+    spec = down((rows, d))
+    return call("start", identity, 8, body, [x], [spec], [like(x.shape)], [spec], [], traffic, times)
+
+
+def gate_up(a, w_gate, w_up, identity, traffic, times):
+    tokens, d = a.shape
+    ff = w_gate.shape[1]
+    cut = tokens // 4
+
+    def body(step, ins, outs, _):
+        a, w_gate, w_up = ins
+        hidden, by_gate, by_up = outs
+        for i in range(0, tokens, cut):
+            rows = pl.ds(i, cut)
+            gate = dot(a[rows, :], w_gate[...])
+            up = dot(a[rows, :], w_up[...])
+            sigmoid = 1.0 / (1.0 + jnp.exp(-gate))
+            silu = gate * sigmoid
+            hidden[rows, :] = (silu * up).astype(BF)
+            by_gate[rows, :] = up * (sigmoid + silu * (1.0 - sigmoid))
+            by_up[rows, :] = silu
+
+    out = along((tokens, WIDE))
+    return call(
+        "gate_up",
+        identity,
+        ff // WIDE,
+        body,
+        [a, w_gate, w_up],
+        [fixed(a.shape)] + [along((d, WIDE))] * 2,
+        [like((tokens, ff)), like((tokens, ff), F32), like((tokens, ff), F32)],
+        [out] * 3,
+        [],
+        traffic,
+        times,
+    )
+
+
+def back_down(h, hidden, w_down, identity, traffic, times):
+    tokens, d = h.shape
+    ff = hidden.shape[1]
+
+    def body(step, ins, outs, _):
+        h, hidden, w_down = ins
+        states = h[...] + dot(hidden[...], w_down[...]).astype(BF)
+        outs[0][...] = states
+        outs[1][...] = normed(states)
+
+    return call(
+        "down",
+        identity,
+        tokens // TALL,
+        body,
+        [h, hidden, w_down],
+        [down((TALL, d)), down((TALL, ff)), fixed(w_down.shape)],
+        [like(h.shape)] * 2,
+        [down((TALL, d))] * 2,
+        [],
+        traffic,
+        times,
+    )
+
+
+def by_hidden(by_h, hidden, by_gate, by_up, w_down, identity, traffic, times):
+    tokens, d = by_h.shape
+    ff = hidden.shape[1]
+    cut = tokens // 4
+
+    def body(step, ins, outs, _):
+        by_h, hidden, by_gate, by_up, w_down = ins
+        gate, up, term = outs
+        for i in range(0, tokens, cut):
+            rows = pl.ds(i, cut)
+            wide = dot(by_h[rows, :], w_down[...], (1, 1)).astype(BF).astype(F32)
+            gate[rows, :] = (wide * by_gate[rows, :]).astype(BF)
+            up[rows, :] = (wide * by_up[rows, :]).astype(BF)
+        term[...] = dot(hidden[...], by_h[...], (0, 0)).astype(BF)
+
+    block = along((tokens, WIDE))
+    return call(
+        "by_hidden",
+        identity,
+        ff // WIDE,
+        body,
+        [by_h, hidden, by_gate, by_up, w_down],
+        [fixed(by_h.shape), block, block, block, down((WIDE, d))],
+        [like((tokens, ff))] * 2 + [like((ff, d))],
+        [block, block, down((WIDE, d))],
+        [],
+        traffic,
+        times,
+    )
+
+
+def by_weights(a, gate, up, identity, traffic, times):
+    tokens, d = a.shape
+    ff = gate.shape[1]
+
+    def body(step, ins, outs, scratch):
+        a, gate, up = ins
+        turned = scratch[0]
+
+        @pl.when(step == 0)
+        def _():
+            for i in range(0, tokens, 256):
+                turned[:, i : i + 256] = a[i : i + 256, :].T
+
+        outs[0][...] = dot(turned[...], gate[...]).astype(BF)
+        outs[1][...] = dot(turned[...], up[...]).astype(BF)
+
+    block = along((tokens, WIDE))
+    return call(
+        "by_weights",
+        identity,
+        ff // WIDE,
+        body,
+        [a, gate, up],
+        [fixed(a.shape), block, block],
+        [like((d, ff))] * 2,
+        [along((d, WIDE))] * 2,
+        [pltpu.VMEM((d, tokens), BF)],
+        traffic,
+        times,
+    )
+
+
+def by_states(h, by_h, gate, up, w_gate, w_up, identity, traffic, times):
+    tokens, d = h.shape
+    ff = gate.shape[1]
+
+    def body(step, ins, outs, _):
+        h, by_h, gate, up, w_gate, w_up = ins
+        by_a = dot(gate[...], w_gate[...], (1, 1)).astype(BF) + dot(up[...], w_up[...], (1, 1)).astype(BF)
+        by_a, wide = by_a.astype(F32), h[...].astype(F32)
+        scale = lax.rsqrt(jnp.mean(wide**2, -1, keepdims=True) + 1e-6)
+        by_wide = scale * by_a - wide * (scale * scale * scale * jnp.mean(by_a * wide, -1, keepdims=True))
+        outs[0][...] = by_h[...] + by_wide.astype(BF)
+
+    states, block = down((TALL, d)), down((TALL, ff))
+    return call(
+        "by_states",
+        identity,
+        tokens // TALL,
+        body,
+        [h, by_h, gate, up, w_gate, w_up],
+        [states, states, block, block, fixed(w_gate.shape), fixed(w_up.shape)],
+        [like(h.shape)],
+        [states],
+        [],
+        traffic,
+        times,
+    )
 
 
 def scatter_all(terms, identity):
@@ -314,23 +570,6 @@
     )(*gradients)
 
 
-def matmul(a, w):
-    return jnp.dot(a, w, preferred_element_type=F32).astype(BF)
-
-
-def normed(h):
-    wide = h.astype(F32)
-    scale = lax.rsqrt(jnp.mean(wide**2, -1, keepdims=True) + 1e-6)
-    return (wide * scale).astype(BF)
-
-
-def layer(h, w):
-    a = normed(h)
-    gate = jnp.dot(a, w["w_gate"], preferred_element_type=F32)
-    up = jnp.dot(a, w["w_up"], preferred_element_type=F32)
-    return h + matmul((jax.nn.silu(gate) * up).astype(BF), w["w_down"])
-
-
 def adamw(w, m, v, g):
     m = 0.9 * m + 0.1 * g
     v = 0.95 * v + 0.05 * g * g
@@ -341,19 +580,24 @@
 def solution(mesh):
     def step(x, dy, *arrays):
         weights, m, v = (arrays[i : i + 3] for i in (0, 3, 6))
-        layers = weights[0].shape[0]
-        whole = gather_all(weights, 0)
-        h, kept = x[0], []
-        for number in range(layers):
-            kept.append(h)
-            h = layer(h, whole[number])
-        by_h, mine = dy[0], [None] * layers
-        for number in reversed(range(layers)):
-            _, back = jax.vjp(lambda w, h: layer(h, w), whole[number], kept[number])
-            by_w, by_h = back(by_h)
-            mine[number] = scatter_all([by_w[name] for name in NAMES], 1 + number)
-        squares = jnp.sum(sum_of_squares([g for one in mine for g in one], 1 + layers))
-        gradients = [jnp.stack([mine[number][i] for number in range(layers)]).astype(F32) for i in range(3)]
+        w_gate, w_up, w_down = weights
+        layers = w_gate.shape[0]
+        x, dy = x[0], dy[0]
+        a0, (wg0, wu0) = start(x, 0, Gathers((w_gate, w_up), [(0, 0), (1, 0)]), [(0, 1, 2, 3, 8), (1, 2, 3, 8, 9)])
+        hid0, g0, u0, (wd0, wg1) = gate_up(
+            a0, wg0, wu0, 1, Gathers((w_down, w_gate), [(0, 0), (1, 1)]), [(0, 2, 5, 9, 13), (1, 4, 8, 13, 14)]
+        )
+        h1, a1, (wu1,) = back_down(x, hid0, wd0, 2, Gathers((w_up,), [(0, 1)]), [(0, 2, 4, 8, 9)])
+        hid1, g1, u1, (wd1,) = gate_up(a1, wg1, wu1, 3, Gathers((w_down,), [(0, 1)]), [(0, 2, 5, 10, 13)])
+        dg1, du1, term_d1, _ = by_hidden(dy, hid1, g1, u1, wd1, 4, Nothing, ())
+        term_g1, term_u1, (d1,) = by_weights(a1, dg1, du1, 5, Scatters([term_d1]), [(0, 3, 8, 11, 13)])
+        by_h1, (sg1,) = by_states(h1, dy, dg1, du1, wg1, wu1, 6, Scatters([term_g1]), [(0, 2, 5, 7, 8)])
+        dg0, du0, term_d0, (su1,) = by_hidden(by_h1, hid0, g0, u0, wd0, 7, Scatters([term_u1]), [(0, 3, 8, 11, 13)])
+        term_g0, term_u0, (d0,) = by_weights(a0, dg0, du0, 8, Scatters([term_d0]), [(0, 3, 8, 11, 13)])
+        sg0, su0 = scatter_all([term_g0, term_u0], 9)
+        mine = [(sg0, sg1), (su0, su1), (d0, d1)]
+        squares = jnp.sum(sum_of_squares([g for pair in mine for g in pair], 10))
+        gradients = [jnp.stack(pair).astype(F32) for pair in mine]
         factor = jnp.minimum(1.0, 0.5 * lax.rsqrt(squares / (16 * sum(g.size for g in gradients)) + 1e-30))
         new = [adamw(w.astype(F32), m, v, g * factor) for w, m, v, g in zip(weights, m, v, gradients, strict=True)]
         return tuple(one[which] for which in range(3) for one in new)

time: 720 us -> 490 us (0.68)
  matrix products: 374 us -> 0 us
  Pallas kernels: 301 us -> 475 us
  local copies, waits for them, and re-layouts: 13.1 us -> 1.27 us
  other arithmetic: 21.3 us -> 10.9 us
    dot_general x15 -> x0, matrix products: 374 us -> none  [the longest x5 135 us: layer(): gate = jnp.dot(a, w['w_gate'], preferred_element_type=F32)]
    pallas_call x1 -> x9, Pallas kernels: 141 us -> 413 us  [call(): pl.pallas_call(kernel, name=name, grid=(steps,), in_specs=in_specs + traf...]
    pallas_call x2 -> x1, Pallas kernels: 151 us -> 53 us  [scatter_all(): pl.pallas_call(kernel, in_specs=[ANY] * n, out_specs=[VMEM] * n, out_shap...]
    unnamed x42 -> x26, local copies, waits for them, and re-layouts: 13.1 us -> 1.27 us
    add_any x1 -> x0, other arithmetic: 7.62 us -> none  [normed(): wide = h.astype(F32)]
where the time goes in v2:
time: 490 us; the launch traced here: 489 us
  Pallas kernels  475 us (97%)
  other arithmetic  10.9 us (2%)
    pallas_call x9, Pallas kernels, call(): pl.pallas_call(kernel, name=name, grid=(steps,), in_specs=in_specs + traf...  413 us
    pallas_call x1, Pallas kernels, scatter_all(): pl.pallas_call(kernel, in_specs=[ANY] * n, out_specs=[VMEM] * n, out_shap...  53 us
    pallas_call x1, Pallas kernels, sum_of_squares(): pl.pallas_call(kernel, in_specs=[VMEM] * n, out_specs=VMEM, out_shape=jax...  9.84 us

profile of v2, /device:TPU:0, one launch (start us, length us, event | category | flops | bytes accessed | tf_op | source)
XLA Modules:
  0.0 489.2 jit_solution(14198349636550537187)
XLA Ops:
  0.6 54.4 %start.1 = (bf16[2048,1024]{1,0:T(8,128)(2,1)}, bf16[2,2,2,2,64,3328]{5,4,3,2,1,0:T(8,128)(2,1)}, bf16[2,2,2,2,64,3328]{5,4,3,2,1,0:T(8,128)(2,1)}) custom-call(bf16[2048,1024]{1,0:T(8,128)(2,1)} %bitcast.26, bf16[2,64,3328]{2,1,0:T(8,128)(2,1)} %refs_4_.1, bf16[2,64,3328]{2,1,0:T(8,128)(2,1)} %refs_3_.4), custom_call_target="tpu_custom_call" | custom-call | tf_op jit(solution)/shard_map/start/pallas_call | solution.py:306
  55.1 57.3 %gate_up.2 = (bf16[2048,3328]{1,0:T(8,128)(2,1)}, f32[2048,3328]{1,0:T(8,128)}, f32[2048,3328]{1,0:T(8,128)}, bf16[2,2,2,2,208,1024]{5,4,3,2,1,0:T(8,128)(2,1)}, bf16[2,2,2,2,64,3328]{5,4,3,2,1,0:T(8,128)(2,1)}) custom-call(bf16[2048,1024]{1,0:T(8,128)(2,1)} %get-tuple-element.41.refs_0_, bf16[1024,3328]{1,0:T(8,128)(2,1)} %bitcast.36, ...), custom_call_target="tpu_custom_call" | custom-call | tf_op jit(solution)/shard_map/gate_up/pallas_call | solution.py:306
  112.3 35.9 %down.1 = (bf16[2048,1024]{1,0:T(8,128)(2,1)}, bf16[2048,1024]{1,0:T(8,128)(2,1)}, bf16[2,2,2,2,64,3328]{5,4,3,2,1,0:T(8,128)(2,1)}) custom-call(bf16[2048,1024]{1,0:T(8,128)(2,1)} %bitcast.27, bf16[2048,3328]{1,0:T(8,128)(2,1)} %get-tuple-element.44.refs_1_, bf16[3328,1024]{1,0:T(8,128)(2,1)} %bitcast.24, bf16[2,64,3328]{2,1,0:T(8,128)(2,1)} %refs_3_.4), custom_call_target="tpu_custom_call" | custom-call | tf_op jit(solution)/shard_map/down/pallas_call | solution.py:306
  148.3 43.8 %gate_up.3 = (bf16[2048,3328]{1,0:T(8,128)(2,1)}, f32[2048,3328]{1,0:T(8,128)}, f32[2048,3328]{1,0:T(8,128)}, bf16[2,2,2,2,208,1024]{5,4,3,2,1,0:T(8,128)(2,1)}) custom-call(bf16[2048,1024]{1,0:T(8,128)(2,1)} %get-tuple-element.47.refs_0_, bf16[1024,3328]{1,0:T(8,128)(2,1)} %bitcast.20, bf16[1024,3328]{1,0:T(8,128)(2,1)} %bitcast.22, ...), custom_call_target="tpu_custom_call" | custom-call | tf_op jit(solution)/shard_map/gate_up/pallas_call | solution.py:306
  192.1 44.1 %by_hidden.2 = (bf16[2048,3328]{1,0:T(8,128)(2,1)}, bf16[2048,3328]{1,0:T(8,128)(2,1)}, bf16[3328,1024]{1,0:T(8,128)(2,1)}) custom-call(bf16[2048,1024]{1,0:T(8,128)(2,1)} %bitcast.28, bf16[2048,3328]{1,0:T(8,128)(2,1)} %get-tuple-element.50.refs_1_, f32[2048,3328]{1,0:T(8,128)} %get-tuple-element.51.refs_2_, f32[2048,3328]{1,0:T(8,128)} %get-tuple-element.52.refs_3_, ...), custom_call_target="tpu_custom_call" | custom-call | tf_op jit(solution)/shard_map/by_hidden/pallas_call | solution.py:306
  236.1 42.4 %by_weights.2 = (bf16[1024,3328]{1,0:T(8,128)(2,1)}, bf16[1024,3328]{1,0:T(8,128)(2,1)}, bf16[208,1024]{1,0:T(8,128)(2,1)}) custom-call(bf16[2048,1024]{1,0:T(8,128)(2,1)} %get-tuple-element.47.refs_0_, bf16[2048,3328]{1,0:T(8,128)(2,1)} %get-tuple-element.54.refs_1_.refs_2_, bf16[2048,3328]{1,0:T(8,128)(2,1)} %get-tuple-element.55.refs_2_.refs_3_, ...), custom_call_target="tpu_custom_call" | custom-call | tf_op jit(solution)/shard_map/by_weights/pallas_call | solution.py:306
  278.5 43.7 %by_states.1 = (bf16[2048,1024]{1,0:T(8,128)(2,1)}, bf16[64,3328]{1,0:T(8,128)(2,1)}) custom-call(bf16[2048,1024]{1,0:T(8,128)(2,1)} %get-tuple-element.46.refs_0_, bf16[2048,1024]{1,0:T(8,128)(2,1)} %bitcast.29, bf16[2048,3328]{1,0:T(8,128)(2,1)} %get-tuple-element.54.refs_1_.refs_2_, bf16[2048,3328]{1,0:T(8,128)(2,1)} %get-tuple-element.55.refs_2_.refs_3_, ...), custom_call_target="tpu_custom_call" | custom-call | tf_op jit(solution)/shard_map/by_states/pallas_call | solution.py:306
  322.2 48.9 %by_hidden.3 = (bf16[2048,3328]{1,0:T(8,128)(2,1)}, bf16[2048,3328]{1,0:T(8,128)(2,1)}, bf16[3328,1024]{1,0:T(8,128)(2,1)}, bf16[64,3328]{1,0:T(8,128)(2,1)}) custom-call(bf16[2048,1024]{1,0:T(8,128)(2,1)} %get-tuple-element.58.refs_0_, bf16[2048,3328]{1,0:T(8,128)(2,1)} %get-tuple-element.44.refs_1_, f32[2048,3328]{1,0:T(8,128)} %get-tuple-element.59.refs_2_, ...), custom_call_target="tpu_custom_call" | custom-call | tf_op jit(solution)/shard_map/by_hidden/pallas_call | solution.py:306
  371.1 42.2 %by_weights.3 = (bf16[1024,3328]{1,0:T(8,128)(2,1)}, bf16[1024,3328]{1,0:T(8,128)(2,1)}, bf16[208,1024]{1,0:T(8,128)(2,1)}) custom-call(bf16[2048,1024]{1,0:T(8,128)(2,1)} %get-tuple-element.41.refs_0_, bf16[2048,3328]{1,0:T(8,128)(2,1)} %get-tuple-element.62.refs_1_, bf16[2048,3328]{1,0:T(8,128)(2,1)} %get-tuple-element.63.refs_2_, ...), custom_call_target="tpu_custom_call" | custom-call | tf_op jit(solution)/shard_map/by_weights/pallas_call | solution.py:306
  413.3 0.0 copy-start.5
  413.3 0.0 copy-start.9
  413.3 53.0 %shard_map.178 = (bf16[64,3328]{1,0:T(8,128)(2,1)}, bf16[64,3328]{1,0:T(8,128)(2,1)}) custom-call(bf16[2,2,2,2,64,3328]{5,4,3,2,1,0:T(8,128)(2,1)} %bitcast.34, bf16[2,2,2,2,64,3328]{5,4,3,2,1,0:T(8,128)(2,1)} %bitcast.35), custom_call_target="tpu_custom_call" | custom-call | tf_op jit(solution)/shard_map/pallas_call | solution.py:510
  466.3 0.0 copy-start
  466.3 0.0 copy-start.3
  466.4 9.8 %shard_map.179 = f32[8,128]{1,0:T(8,128)} custom-call(bf16[64,3328]{1,0:T(8,128)(2,1)} %get-tuple-element.67.refs_0_, bf16[64,3328]{1,0:T(8,128)(2,1)} %get-tuple-element.68.refs_1_, bf16[64,3328]{1,0:T(8,128)(2,1)} %get-tuple-element.69.refs_2_, bf16[64,3328]{1,0:T(8,128)(2,1)} %get-tuple-element.70.refs_3_, bf16[208,1024]{1,0:T(8,128)(2,1)} %get-tuple-element.71.refs_4_, ...), custom_call_target="tpu_custom_call" | custom-call | tf_op jit(solution)/shard_map/pallas_call | solution.py:563
  476.2 1.3 reduce_sum.9
  478.2 0.0 copy-done.5
  478.2 0.0 copy-done.9
  478.2 0.0 copy-done
  478.2 0.0 copy-done.3
  478.2 0.0 copy-start.1
  478.2 0.0 copy-start.2
  478.2 0.0 copy-start.4
  478.3 0.0 copy-start.6
  478.3 0.0 copy-start.10
  478.3 0.0 copy-start.11
  478.3 0.0 copy-start.12
  478.3 4.2 fusion.8
  482.5 0.0 copy-done.1
  482.6 0.1 copy-done.11
  482.7 1.1 copy-done.12
  483.8 5.4 %fusion.2 = (bf16[2,64,3328]{2,1,0:T(8,128)(2,1)}, f32[2,64,3328]{2,1,0:T(8,128)}, f32[2,64,3328]{2,1,0:T(8,128)}, bf16[2,64,3328]{2,1,0:T(8,128)(2,1)}, f32[2,64,3328]{2,1,0:T(8,128)}, /*index=5*/f32[2,64,3328]{2,1,0:T(8,128)}) fusion(bf16[2,64,3328]{2,1,0:T(8,128)(2,1)S(1)} %copy-done.1, f32[]{:T(128)S(6)} %min_shard_map.3, ...), kind=kLoop, calls=%fused_computation.11 | loop fusion | flops 17039360 | bytes 18743300 | tf_op jit(solution)/shard_map/convert_element_type | solution.py:577
  (8 shorter events, 0.0 us)
Async XLA Ops:
  413.3 64.9 %copy-start.5 = (bf16[208,1024]{1,0:T(8,128)(2,1)S(1)}, bf16[208,1024]{1,0:T(8,128)(2,1)}, u32[]{:S(2)}) copy-start(bf16[208,1024]{1,0:T(8,128)(2,1)} %get-tuple-element.72.refs_5_) | copy-start | bytes 1277956
  413.3 64.9 %copy-start.9 = (bf16[208,1024]{1,0:T(8,128)(2,1)S(1)}, bf16[208,1024]{1,0:T(8,128)(2,1)}, u32[]{:S(2)}) copy-start(bf16[208,1024]{1,0:T(8,128)(2,1)} %get-tuple-element.71.refs_4_) | copy-start | bytes 1277956
  466.3 11.9 %copy-start = (bf16[2,208,1024]{2,1,0:T(8,128)(2,1)S(1)}, bf16[2,208,1024]{2,1,0:T(8,128)(2,1)}, u32[]{:S(2)}) copy-start(bf16[2,208,1024]{2,1,0:T(8,128)(2,1)} %refs_3_.5) | copy-start | bytes 2555908
  466.3 11.9 %copy-start.3 = (f32[2,208,1024]{2,1,0:T(8,128)S(1)}, f32[2,208,1024]{2,1,0:T(8,128)}, u32[]{:S(2)}) copy-start(f32[2,208,1024]{2,1,0:T(8,128)} %param.21) | copy-start | bytes 5111812
  478.2 4.3 copy-start.1
  478.2 4.3 copy-start.2
  478.2 4.3 copy-start.4
  478.3 4.3 copy-start.6
  478.3 4.3 copy-start.7
  478.3 4.3 copy-start.8
  478.3 4.3 copy-start.10
  478.3 4.4 copy-start.11
  478.3 5.5 %copy-start.12 = (f32[2,64,3328]{2,1,0:T(8,128)S(1)}, f32[2,64,3328]{2,1,0:T(8,128)}, u32[]{:S(2)}) copy-start(f32[2,64,3328]{2,1,0:T(8,128)} %param.20) | copy-start | bytes 5111812
